TPU v7x, 32 devices: a whole 2x2x4 slice. The times are simulated.
32 devices in a mesh: row: 4 (over y, x), col: 8 (over z, core).
Axes of the slice: x: 2, y: 2, z: 4, core: 2. Of those that a mesh axis runs over, the one named last changes fastest.
Arguments:
- density: bfloat16 [2048, 2048], P('row', 'col'), may hold values from -0.125 to 0.125
- density_mask: int32 [16, 16], P('row', 'col'), may hold values from 0 to 1, as said below
- response: bfloat16 [2, 2048, 2048], P(None, 'row', 'col'), may hold values from -6 to 6
- response_mask: int32 [2, 16, 16], P(None, 'row', 'col'), may hold values from 0 to 1, as said below
- filter_mask: int32 [16, 16], P('row', 'col'), may hold values from 0 to 1, as said below
Outputs:
- product: bfloat16 [2, 2048, 2048], P(None, 'row', 'col')
Inputs may be any that keep to these rules, and one draw needn't show every extreme that they name: `density_mask`: diagonal blocks are always nonzero; blocks within cyclic block distance 2 of the diagonal are more often nonzero than blocks further out; whole block rows and whole block columns may be nonzero. `response_mask`: for each direction, diagonal blocks are always nonzero; blocks within cyclic block distance 2 of the diagonal are more often nonzero than blocks further out; whole block rows and whole block columns may be nonzero. `filter_mask`: diagonal blocks are always kept; blocks within cyclic block distance 2 * 2 of the diagonal are more often kept than blocks further out; whole block rows and whole block columns may be kept.
All inputs are finite; a program needn't handle non-finite values.
Results may differ from a plain program's by a relative error of at most 0.001.
Values may be sent and summed in bfloat16 or wider, within the bound.
A program may use at most 128 MiB of HBM per device.

v0:
```python
import jax
import jax.numpy as jnp
from jax import lax
from jax.sharding import PartitionSpec as P


def expand_blocks(values, mask, blocksize):
    lead = values.shape[:-2]
    height = values.shape[-2] // blocksize
    width = values.shape[-1] // blocksize
    shaped = values.reshape(lead + (height, blocksize, width, blocksize))
    scaled = shaped * mask.astype(values.dtype)[..., :, None, :, None]
    return scaled.reshape(values.shape)


def body(density, density_mask, response, response_mask, filter_mask):
    blocksize = density.shape[1] // density_mask.shape[1]
    masked_density = expand_blocks(density, density_mask, blocksize)
    masked_response = expand_blocks(response, response_mask, blocksize)
    density_full = lax.all_gather(masked_density, "col", axis=1, tiled=True)
    result = jnp.einsum(
        "ik,dkj->dij",
        density_full,
        lax.all_gather(masked_response, "row", axis=1, tiled=True),
        preferred_element_type=jnp.float32,
    )
    return expand_blocks(result, filter_mask, blocksize).astype(jnp.bfloat16)


def solution(mesh):
    in_specs = (
        P("row", "col"),
        P("row", "col"),
        P(None, "row", "col"),
        P(None, "row", "col"),
        P("row", "col"),
    )
    out_specs = P(None, "row", "col")
    return jax.shard_map(body, mesh=mesh, in_specs=in_specs, out_specs=out_specs, check_vma=False)
```

profile of v0, /device:TPU:1, one launch (start us, length us, event | category | flops | bytes accessed | tf_op | source)
XLA Modules:
  0.0 91.1 jit_solution(6940822390799597102)
XLA Ops:
  6.5 0.0 all-gather.3.cloned.1.call-start
  6.5 0.7 convert_element_type.12
  7.2 0.2 mul.35
  7.4 0.0 copy-start.2
  7.4 0.0 copy-start
  7.5 0.2 mul.36
  7.7 0.0 copy-start.1
  7.7 1.3 %copy.6 = bf16[2,512,256]{1,2,0:T(8,128)(2,1)S(1)} copy(bf16[2,512,256]{2,1,0:T(8,128)(2,1)} %param.7) | data formatting | bytes 1048576 | tf_op args[2]
  8.9 0.9 %mul.37 = bf16[2,512,256]{1,2,0:T(8,128)(2,1)} multiply(bf16[2,512,256]{1,2,0:T(8,128)(2,1)S(1)} %copy.6, bf16[2,512,256]{1,2,0:T(8,128)(2,1)S(1)} %mul.36) | non-fusion elementwise | flops 262144 | bytes 1572864 | tf_op jit(solution)/shard_map/mul | solution.py:12
  9.9 0.0 all-gather.3.cloned.1.call-update
  9.9 0.0 all-gather.5.cloned.1.call-start
  9.9 0.0 copy-done.2
  10.0 0.1 copy.7
  10.1 0.2 mul.38
  10.3 0.0 copy-done
  10.3 0.8 bitcast_multiply_fusion
  11.0 0.0 all-gather.5.cloned.1.call-update
  11.1 0.0 copy-done.1
  11.1 0.1 mul.41
  11.3 35.7 %all-gather.3.cloned.1.call-done = bf16[2,2048,256]{1,2,0:T(8,128)(2,1)} async-done(((bf16[2,512,256]{1,2,0:T(8,128)(2,1)}), bf16[2,2048,256]{1,2,0:T(8,128)(2,1)}) %all-gather.3.cloned.1.call-update) | async-done | bytes 2097168 | tf_op jit(solution)/shard_map/all_gather | solution.py:24
  47.0 32.8 %all-gather.5.cloned.1.call-done = bf16[512,2048]{1,0:T(8,128)(2,1)} async-done(((bf16[512,256]{1,0:T(8,128)(2,1)}), bf16[512,2048]{1,0:T(8,128)(2,1)}) %all-gather.5.cloned.1.call-update) | async-done | bytes 2097168 | tf_op jit(solution)/shard_map/all_gather | solution.py:20
  79.8 3.5 %fusion.8 = bf16[2,512,256]{1,2,0:T(8,128)(2,1)S(1)} fusion(bf16[2,2048,256]{1,2,0:T(8,128)(2,1)} %all-gather.3.cloned.1.call-done, bf16[512,2048]{1,0:T(8,128)(2,1)} %all-gather.5.cloned.1.call-done, f32[512,256]{0,1:T(8,128)S(1)} %bitcast.31), kind=kOutput, calls=%fused_computation.4 | convolution fusion | flops 1074266112 | bytes 5242880 | tf_op jit(solution)/shard_map/ik,dkj->dij/dot_general | solution.py:21
  83.3 1.0 %copy.8 = bf16[2,512,256]{2,1,0:T(8,128)(2,1)} copy(bf16[2,512,256]{1,2,0:T(8,128)(2,1)S(1)} %fusion.8) | data formatting | bytes 1048576 | tf_op jit(solution)/shard_map/convert_element_type | solution.py:27
  (3 shorter events, 0.0 us)
Async XLA Ops:
  6.5 40.5 %all-gather.3.cloned.1.call-start = ((), (), s32[]{:S(2)}) async-start(), calls=%async_computation | async-start | bytes 2621440 | tf_op jit(solution)/shard_map/all_gather | solution.py:24
  7.4 2.5 %copy-start.2 = (s32[4,2]{0,1:T(2,128)S(1)}, s32[4,2]{0,1:T(2,128)}, u32[]{:S(2)}) copy-start(s32[4,2]{0,1:T(2,128)} %param.6) | copy-start | bytes 100
  7.4 2.8 %copy-start = (bf16[512,256]{1,0:T(8,128)(2,1)S(1)}, bf16[512,256]{1,0:T(8,128)(2,1)}, u32[]{:S(2)}) copy-start(bf16[512,256]{1,0:T(8,128)(2,1)} %param.5) | copy-start | bytes 786436
  7.7 3.4 %copy-start.1 = (s32[4,2]{0,1:T(2,128)S(1)}, s32[4,2]{0,1:T(2,128)}, u32[]{:S(2)}) copy-start(s32[4,2]{0,1:T(2,128)} %param.9) | copy-start | bytes 100
  9.9 69.9 %all-gather.5.cloned.1.call-start = ((), (), s32[]{:S(2)}) async-start(), calls=%async_computation.1 | async-start | bytes 2359296 | tf_op jit(solution)/shard_map/all_gather | solution.py:20
Sparse Core Ops, SparseCore 0:
  10.0 36.9 all-gather.2
  48.6 31.1 all-gather.4
where the time goes:
time: 92.2 us; the launch traced here: 91.1 us
  waiting for transfers between devices  68.5 us (74%)
  between operations  13.5 us (15%)
  matrix products  3.5 us (4%)
  local copies, waits for them, and re-layouts  3.17 us (3%)
  other arithmetic  2.37 us (3%)
    all_gather x1, waiting for transfers between devices, body(): lax.all_gather(masked_response, 'row', axis=1, tiled=True)  35.7 us
    all_gather x1, waiting for transfers between devices, body(): density_full = lax.all_gather(masked_density, 'col', axis=1, tiled=True)  32.8 us
    dot_general x1, matrix products, body(): jnp.einsum('ik,dkj->dij', density_full, lax.all_gather(masked_response, '...  3.5 us
  transfers between devices with their start and end apart: 2, of which 2 were waited for; matrix products, arithmetic and copies ran while one was open for 1% of the time, Pallas kernels for 0%

commit v1 on v0

v1 whole, which is shorter than its diff:
```python
import functools

import jax
import jax.numpy as jnp
from jax import lax
from jax.experimental import pallas as pl
from jax.experimental.pallas import tpu as pltpu
from jax.sharding import PartitionSpec as P

CORES = 2
HALVES = 2


def kernel(
    ring, cols, density, density_mask, response, response_mask, filter_mask,
    out, a_full, b_full, acc, load_sem,
    a_send, a_recv, b_send, b_recv, d_send, d_recv,
):
    chips = cols // CORES
    dirs, depth, width = response.shape
    rows, kblock = density.shape
    piece = rows // HALVES
    per = depth // kblock
    nb = dirs * per
    far = ring // 2
    a_items = HALVES * (chips - 1)
    b_items = nb * (far - 1) + nb // 2
    blk_r = rows // density_mask.shape[0]
    blk_k = kblock // density_mask.shape[1]

    row = lax.axis_index("row")
    col = lax.axis_index("col")
    chip, core = col // CORES, col % CORES
    partner = chip * CORES + (CORES - 1 - core)

    def row_of(pos):
        pos = lax.rem(pos + 2 * ring, ring)
        return jnp.where(pos < far, 2 * pos, 2 * (ring - 1 - pos) + 1)

    def pos_of(r):
        return jnp.where(r % 2 == 0, r // 2, ring - 1 - r // 2)

    pos = pos_of(row)
    next_row, prev_row = row_of(pos + 1), row_of(pos - 1)
    has_up, has_down = chip < chips - 1, chip > 0

    barrier = pltpu.get_barrier_semaphore()
    pl.semaphore_signal(barrier, inc=1, device_id={"row": next_row})
    pl.semaphore_signal(barrier, inc=1, device_id={"row": prev_row})
    pl.semaphore_signal(barrier, inc=1, device_id={"col": partner})

    @pl.when(has_up)
    def _():
        pl.semaphore_signal(barrier, inc=1, device_id={"col": col + CORES})

    @pl.when(has_down)
    def _():
        pl.semaphore_signal(barrier, inc=1, device_id={"col": col - CORES})

    load_a = pltpu.make_async_copy(density, a_full.at[col], load_sem.at[0])
    load_b = pltpu.make_async_copy(response, b_full.at[row], load_sem.at[1])
    load_a.start()
    load_b.start()
    acc[...] = jnp.zeros_like(acc)
    load_a.wait()
    for i in range(rows // blk_r):
        for k in range(kblock // blk_k):
            part = (col, pl.ds(i * blk_r, blk_r), pl.ds(k * blk_k, blk_k))
            factor = jnp.full((blk_r, blk_k), density_mask[i, k].astype(jnp.float32)).astype(jnp.bfloat16)
            a_full[part] = a_full[part] * factor
    load_b.wait()
    for d in range(dirs):
        for i in range(depth // blk_k):
            for k in range(width // blk_k):
                part = (row, d, pl.ds(i * blk_k, blk_k), pl.ds(k * blk_k, blk_k))
                factor = jnp.full((blk_k, blk_k), response_mask[d, i, k].astype(jnp.float32)).astype(jnp.bfloat16)
                b_full[part] = b_full[part] * factor
    pl.semaphore_wait(barrier, 3 + has_up.astype(jnp.int32) + has_down.astype(jnp.int32))

    def a_copy(way, item):
        step, half = item // HALVES, item % HALVES
        sign = 1 - 2 * way
        origin = (chip - sign * step) * CORES + core
        ref = a_full.at[origin, pl.ds(pl.multiple_of(half * piece, piece), piece)]
        return pltpu.make_async_remote_copy(
            ref, ref, a_send.at[way, item], a_recv.at[way, item],
            device_id={"col": col + sign * CORES},
        )

    def a_arrival(way, item):
        step, half = item // HALVES, item % HALVES
        sign = 1 - 2 * way
        origin = (chip - sign * (step + 1)) * CORES + core
        ref = a_full.at[origin, pl.ds(pl.multiple_of(half * piece, piece), piece)]
        return pltpu.make_async_remote_copy(
            ref, ref, a_send.at[way, item], a_recv.at[way, item],
            device_id={"col": col + sign * CORES},
        )

    def d_copy(origin_chip, half, whose):
        ref = a_full.at[origin_chip * CORES + whose, pl.ds(pl.multiple_of(half * piece, piece), piece)]
        return pltpu.make_async_remote_copy(
            ref, ref, d_send.at[origin_chip, half], d_recv.at[origin_chip, half],
            device_id={"col": partner},
        )

    def b_ref(way, item, origin_pos):
        j = item % nb
        d, s = j // per, j % per
        if way == 1:
            d = dirs - 1 - d
        return b_full.at[row_of(origin_pos), d, pl.ds(pl.multiple_of(s * kblock, kblock), kblock)]

    def b_copy(way, item):
        sign = 1 - 2 * way
        ref = b_ref(way, item, pos - sign * (item // nb))
        return pltpu.make_async_remote_copy(
            ref, ref, b_send.at[way, item], b_recv.at[way, item],
            device_id={"row": next_row if way == 0 else prev_row},
        )

    def b_arrival(way, item):
        sign = 1 - 2 * way
        ref = b_ref(way, item, pos - sign * (item // nb + 1))
        return pltpu.make_async_remote_copy(
            ref, ref, b_send.at[way, item], b_recv.at[way, item],
            device_id={"row": next_row if way == 0 else prev_row},
        )

    own_b = min(nb, b_items)
    for item in range(max(own_b, HALVES)):
        if item < HALVES and chips > 1:
            pl.when(has_up)(lambda item=item: a_copy(0, item).start())
            pl.when(has_down)(lambda item=item: a_copy(1, item).start())
        if item < own_b:
            b_copy(0, item).start()
            b_copy(1, item).start()
    for half in range(HALVES):
        d_copy(chip, half, core).start()

    def ready(origin_chip, d):
        t_a = HALVES * jnp.abs(origin_chip - chip)
        source = (origin_chip * CORES) // per
        gap = lax.rem(pos - pos_of(source) + ring, ring)
        from_prev = (gap - 1) * nb + (d + 1) * per
        from_next = (ring - gap - 1) * nb + (dirs - d) * per
        up = jnp.logical_or(gap < far, jnp.logical_and(gap == far, d < dirs // 2))
        t_b = jnp.where(gap == 0, 0, jnp.where(up, from_prev, from_next))
        return jnp.maximum(t_a, t_b)

    def compute(tick):
        def unit(index, carry):
            o, d = index // dirs, index % dirs

            @pl.when(ready(o, d) == tick)
            def _():
                source = (o * CORES) // per
                s = (o * CORES) % per
                total = acc[d]
                for c in range(CORES):
                    total += jnp.dot(
                        a_full[o * CORES + c],
                        b_full[source, d, pl.ds(pl.multiple_of((s + c) * kblock, kblock), kblock)],
                        preferred_element_type=jnp.float32,
                    )
                acc[d] = total
            return carry

        lax.fori_loop(0, chips * dirs, unit, 0)

    ticks = max(a_items, b_items)

    def step(tick, carry):
        item = tick - 1

        @pl.when(tick > 0)
        def _():
            for way in range(2):
                sign = 1 - 2 * way
                origin = chip - sign * (item // HALVES + 1)
                here = jnp.logical_and(item < a_items, jnp.logical_and(origin >= 0, origin < chips))

                @pl.when(here)
                def _():
                    a_arrival(way, item).wait_recv()

                    @pl.when(has_up if way == 0 else has_down)
                    def _():
                        a_copy(way, item + HALVES).start()

                    d_copy(origin, item % HALVES, core).start()

            @pl.when(item < b_items)
            def _():
                for way in range(2):
                    b_arrival(way, item).wait_recv()

                    @pl.when(item + nb < b_items)
                    def _():
                        b_copy(way, item + nb).start()

            for way in range(2):
                sign = 1 - 2 * way
                origin = chip - sign * (item // HALVES + 1)
                here = jnp.logical_and(item < a_items, jnp.logical_and(origin >= 0, origin < chips))

                @pl.when(here)
                def _():
                    d_copy(origin, item % HALVES, CORES - 1 - core).wait_recv()

        @pl.when(tick == 0)
        def _():
            for half in range(HALVES):
                d_copy(chip, half, CORES - 1 - core).wait_recv()

        compute(tick)
        return carry

    lax.fori_loop(0, ticks + 1, step, 0)

    blk_m, blk_n = rows // filter_mask.shape[0], width // filter_mask.shape[1]
    for d in range(dirs):
        for i in range(rows // blk_m):
            for k in range(width // blk_n):
                part = (d, pl.ds(i * blk_m, blk_m), pl.ds(k * blk_n, blk_n))
                out[part] = (acc[part] * filter_mask[i, k].astype(jnp.float32)).astype(jnp.bfloat16)

    def drain_a(item, carry):
        for way in range(2):
            sign = 1 - 2 * way
            origin = chip - sign * (item // HALVES)
            sent = jnp.logical_and(has_up if way == 0 else has_down, jnp.logical_and(origin >= 0, origin < chips))
            pl.when(sent)(lambda way=way: a_copy(way, item).wait_send())
        return carry

    def drain_b(item, carry):
        for way in range(2):
            b_copy(way, item).wait_send()
        return carry

    def drain_d(index, carry):
        d_copy(index // HALVES, index % HALVES, core).wait_send()
        return carry

    lax.fori_loop(0, a_items, drain_a, 0)
    lax.fori_loop(0, b_items, drain_b, 0)
    lax.fori_loop(0, chips * HALVES, drain_d, 0)


def solution(mesh):
    ring, cols = mesh.shape["row"], mesh.shape["col"]

    def body(density, density_mask, response, response_mask, filter_mask):
        dirs, depth, width = response.shape
        rows, kblock = density.shape
        chips = cols // CORES
        nb = dirs * (depth // kblock)
        a_items = HALVES * (chips - 1)
        b_items = nb * (ring // 2 - 1) + nb // 2
        dma = pltpu.SemaphoreType.DMA
        hbm = pl.BlockSpec(memory_space=pl.ANY)
        smem = pl.BlockSpec(memory_space=pltpu.SMEM)
        return pl.pallas_call(
            functools.partial(kernel, ring, cols),
            out_shape=jax.ShapeDtypeStruct((dirs, rows, width), jnp.bfloat16),
            in_specs=[hbm, smem, hbm, smem, smem],
            out_specs=pl.BlockSpec(memory_space=pltpu.VMEM),
            scratch_shapes=[
                pltpu.VMEM((cols, rows, kblock), jnp.bfloat16),
                pltpu.VMEM((ring, dirs, depth, width), jnp.bfloat16),
                pltpu.VMEM((dirs, rows, width), jnp.float32),
                dma((2,)),
                dma((2, a_items)),
                dma((2, a_items)),
                dma((2, b_items)),
                dma((2, b_items)),
                dma((chips, HALVES)),
                dma((chips, HALVES)),
            ],
            compiler_params=pltpu.CompilerParams(collective_id=0, has_side_effects=True),
        )(density, density_mask, response, response_mask, filter_mask)

    return jax.shard_map(
        body,
        mesh=mesh,
        in_specs=(P("row", "col"), P("row", "col"), P(None, "row", "col"), P(None, "row", "col"), P("row", "col")),
        out_specs=P(None, "row", "col"),
        check_vma=False,
    )
```

time: 92.2 us -> 31.6 us (0.34)
  waiting for transfers between devices: 68.5 us -> 0 us
  Pallas kernels: 0 us -> 26.8 us
  between operations: 13.5 us -> 0.01 us
  matrix products: 3.5 us -> 0 us
  other arithmetic: 2.37 us -> 0 us
  local copies, waits for them, and re-layouts: 3.17 us -> 4.59 us
    all_gather x2 -> x0, waiting for transfers between devices: 68.5 us -> none  [the longest x1 35.7 us: body(): lax.all_gather(masked_response, 'row', axis=1, tiled=True)]
    pallas_call x0 -> x1, Pallas kernels: none -> 26.8 us  [body(): pl.pallas_call(functools.partial(kernel, ring, cols), out_shape=jax.Shape...]
    dot_general x1 -> x0, matrix products: 3.5 us -> none  [body(): jnp.einsum('ik,dkj->dij', density_full, lax.all_gather(masked_response, '...]
    unnamed x8, local copies, waits for them, and re-layouts: 1.31 us -> 4.59 us
    mul x2 -> x0, other arithmetic: 1.68 us -> none  [expand_blocks(): scaled = shaped * mask.astype(values.dtype)[..., :, None, :, None]]
    convert_element_type x2 -> x0, local copies, waits for them, and re-layouts: 1.11 us -> none  [the longest x1 1 us: body(): return expand_blocks(result, filter_mask, blocksize).astype(jnp.bfloat16)]
  transfers between devices with their start and end apart: 2 -> 0, of which waited for: 2 -> 0; matrix products, arithmetic and copies ran while one was open for 1% -> 0% of each run, Pallas kernels for 0% -> 0%
where the time goes in v1:
time: 31.6 us; the launch traced here: 31.4 us
  Pallas kernels  26.8 us (85%)
  local copies, waits for them, and re-layouts  4.59 us (15%)
    pallas_call x1, Pallas kernels, body(): pl.pallas_call(functools.partial(kernel, ring, cols), out_shape=jax.Shape...  26.8 us
    unnamed x8, local copies, waits for them, and re-layouts  4.59 us

profile of v1, /device:TPU:1, one launch (start us, length us, event | category | flops | bytes accessed | tf_op | source)
XLA Modules:
  0.0 31.4 jit_solution(2148464869059556288)
XLA Ops:
  0.0 0.0 copy-start.1
  0.0 1.3 %copy.6.density_mask = s32[4,2]{1,0:T(4,128)} copy(s32[4,2]{0,1:T(2,128)} %param.6) | data formatting | bytes 64 | tf_op args[1]
  1.4 0.0 copy-done.1
  1.4 0.0 copy-start
  1.4 0.7 %copy.8.filter_mask = s32[4,2]{1,0:T(4,128)} copy(s32[4,2]{0,1:T(2,128)S(1)} %copy-done.1) | data formatting | bytes 64 | tf_op args[4]
  2.0 0.0 copy-done
  2.0 0.7 %copy.7.response_mask = s32[2,4,2]{2,1,0:T(4,128)} copy(s32[2,4,2]{1,2,0:T(2,128)S(1)} %copy-done) | data formatting | bytes 128 | tf_op args[3]
  2.7 26.8 %shard_map.55 = bf16[2,512,256]{2,1,0:T(8,128)(2,1)} custom-call(bf16[512,256]{1,0:T(8,128)(2,1)} %density.1, s32[4,2]{1,0:T(4,128)} %copy.6.density_mask, bf16[2,512,256]{2,1,0:T(8,128)(2,1)} %response.1, s32[2,4,2]{2,1,0:T(4,128)} %copy.7.response_mask, s32[4,2]{1,0:T(4,128)} %copy.8.filter_mask), custom_call_target="tpu_custom_call" | custom-call | tf_op jit(solution)/shard_map/pallas_call | solution.py:263
  29.5 1.9 %copy.10 = bf16[2,512,256]{2,1,0:T(8,128)(2,1)} copy(bf16[2,512,256]{2,1,0:T(8,128)(2,1)} %shard_map.55) | data formatting | bytes 1048576
Async XLA Ops:
  0.0 1.4 %copy-start.1 = (s32[4,2]{0,1:T(2,128)S(1)}, s32[4,2]{0,1:T(2,128)}, u32[]{:S(2)}) copy-start(s32[4,2]{0,1:T(2,128)} %param.9) | copy-start | bytes 100
  1.4 0.7 %copy-start = (s32[2,4,2]{1,2,0:T(2,128)S(1)}, s32[2,4,2]{1,2,0:T(2,128)}, u32[]{:S(2)}) copy-start(s32[2,4,2]{1,2,0:T(2,128)} %param.8) | copy-start | bytes 196

commit v2 on v1

--- a/solution.py
+++ b/solution.py
@@ -25,8 +25,8 @@
     far = ring // 2
     a_items = HALVES * (chips - 1)
     b_items = nb * (far - 1) + nb // 2
-    blk_r = rows // density_mask.shape[0]
-    blk_k = kblock // density_mask.shape[1]
+    blk_r = rows // density_mask.shape[1]
+    blk_k = kblock // density_mask.shape[0]
 
     row = lax.axis_index("row")
     col = lax.axis_index("col")
@@ -66,14 +66,14 @@
     for i in range(rows // blk_r):
         for k in range(kblock // blk_k):
             part = (col, pl.ds(i * blk_r, blk_r), pl.ds(k * blk_k, blk_k))
-            factor = jnp.full((blk_r, blk_k), density_mask[i, k].astype(jnp.float32)).astype(jnp.bfloat16)
+            factor = jnp.full((blk_r, blk_k), density_mask[k, i].astype(jnp.float32)).astype(jnp.bfloat16)
             a_full[part] = a_full[part] * factor
     load_b.wait()
     for d in range(dirs):
         for i in range(depth // blk_k):
             for k in range(width // blk_k):
                 part = (row, d, pl.ds(i * blk_k, blk_k), pl.ds(k * blk_k, blk_k))
-                factor = jnp.full((blk_k, blk_k), response_mask[d, i, k].astype(jnp.float32)).astype(jnp.bfloat16)
+                factor = jnp.full((blk_k, blk_k), response_mask[d, k, i].astype(jnp.float32)).astype(jnp.bfloat16)
                 b_full[part] = b_full[part] * factor
     pl.semaphore_wait(barrier, 3 + has_up.astype(jnp.int32) + has_down.astype(jnp.int32))
 
@@ -218,12 +218,12 @@
 
     lax.fori_loop(0, ticks + 1, step, 0)
 
-    blk_m, blk_n = rows // filter_mask.shape[0], width // filter_mask.shape[1]
+    blk_m, blk_n = rows // filter_mask.shape[1], width // filter_mask.shape[0]
     for d in range(dirs):
         for i in range(rows // blk_m):
             for k in range(width // blk_n):
                 part = (d, pl.ds(i * blk_m, blk_m), pl.ds(k * blk_n, blk_n))
-                out[part] = (acc[part] * filter_mask[i, k].astype(jnp.float32)).astype(jnp.bfloat16)
+                out[part] = (acc[part] * filter_mask[k, i].astype(jnp.float32)).astype(jnp.bfloat16)
 
     def drain_a(item, carry):
         for way in range(2):
@@ -262,7 +262,7 @@
         smem = pl.BlockSpec(memory_space=pltpu.SMEM)
         return pl.pallas_call(
             functools.partial(kernel, ring, cols),
-            out_shape=jax.ShapeDtypeStruct((dirs, rows, width), jnp.bfloat16),
+            out_shape=pltpu.VMEM((dirs, rows, width), jnp.bfloat16),
             in_specs=[hbm, smem, hbm, smem, smem],
             out_specs=pl.BlockSpec(memory_space=pltpu.VMEM),
             scratch_shapes=[
@@ -278,7 +278,7 @@
                 dma((chips, HALVES)),
             ],
             compiler_params=pltpu.CompilerParams(collective_id=0, has_side_effects=True),
-        )(density, density_mask, response, response_mask, filter_mask)
+        )(density, density_mask.T, response, jnp.swapaxes(response_mask, 1, 2), filter_mask.T)
 
     return jax.shard_map(
         body,

time: 31.6 us -> 26.9 us (0.85)
  local copies, waits for them, and re-layouts: 4.59 us -> 0.8 us
  Pallas kernels: 26.8 us -> 25.9 us
    unnamed x8 -> x1, local copies, waits for them, and re-layouts: 4.59 us -> 0.8 us
    pallas_call x1, Pallas kernels: 26.8 us -> 25.9 us  [body(): pl.pallas_call(functools.partial(kernel, ring, cols), out_shape=pltpu.VME...]
where the time goes in v2:
time: 26.9 us; the launch traced here: 26.7 us
  Pallas kernels  25.9 us (96%)
  local copies, waits for them, and re-layouts  0.8 us (3%)
    pallas_call x1, Pallas kernels, body(): pl.pallas_call(functools.partial(kernel, ring, cols), out_shape=pltpu.VME...  25.9 us
    unnamed x1, local copies, waits for them, and re-layouts  0.8 us

profile of v2, /device:TPU:1, one launch (start us, length us, event | category | flops | bytes accessed | tf_op | source)
XLA Modules:
  0.0 26.7 jit_solution(6822334533867110001)
XLA Ops:
  0.0 25.9 %shard_map.55 = bf16[2,512,256]{2,1,0:T(8,128)(2,1)S(1)} custom-call(bf16[512,256]{1,0:T(8,128)(2,1)} %density.1, s32[2,4]{1,0:T(2,128)} %bitcast.4, bf16[2,512,256]{2,1,0:T(8,128)(2,1)} %response.1, s32[2,2,4]{2,1,0:T(2,128)} %bitcast.3, s32[2,4]{1,0:T(2,128)} %bitcast.5), custom_call_target="tpu_custom_call" | custom-call | tf_op jit(solution)/shard_map/pallas_call | solution.py:263
  26.0 0.8 %copy.7 = bf16[2,512,256]{2,1,0:T(8,128)(2,1)} copy(bf16[2,512,256]{2,1,0:T(8,128)(2,1)S(1)} %shard_map.55) | data formatting | bytes 1048576

commit v3 on v2

v3 whole, which is shorter than its diff:
```python
import functools

import jax
import jax.numpy as jnp
from jax import lax
from jax.experimental import pallas as pl
from jax.experimental.pallas import tpu as pltpu
from jax.sharding import PartitionSpec as P

CORES = 2
PIECES = 4
SPLIT = 2


def kernel(
    ring, cols, density, density_mask_in, response, response_mask_in, filter_mask_in,
    out, density_mask, response_mask, filter_mask, a_full, b_full, acc, load_sem,
    a_send, a_recv, b_send, b_recv, d_send, d_recv,
):
    chips = cols // CORES
    dirs, depth, width = response.shape
    rows, kblock = density.shape
    piece = rows // PIECES
    per = depth // kblock
    thin = kblock // SPLIT
    nb = dirs * per * SPLIT
    far = ring // 2
    a_items = PIECES * (chips - 1)
    b_items = nb * (far - 1) + nb // 2
    blk_r = rows // density_mask.shape[1]
    blk_k = kblock // density_mask.shape[0]

    row = lax.axis_index("row")
    col = lax.axis_index("col")
    chip, core = col // CORES, col % CORES
    partner = chip * CORES + (CORES - 1 - core)

    def row_of(pos):
        pos = lax.rem(pos + 2 * ring, ring)
        return jnp.where(pos < far, 2 * pos, 2 * (ring - 1 - pos) + 1)

    def pos_of(r):
        return jnp.where(r % 2 == 0, r // 2, ring - 1 - r // 2)

    pos = pos_of(row)
    next_row, prev_row = row_of(pos + 1), row_of(pos - 1)
    has_up, has_down = chip < chips - 1, chip > 0

    barrier = pltpu.get_barrier_semaphore()
    pl.semaphore_signal(barrier, inc=1, device_id={"row": next_row})
    pl.semaphore_signal(barrier, inc=1, device_id={"row": prev_row})
    pl.semaphore_signal(barrier, inc=1, device_id={"col": partner})

    @pl.when(has_up)
    def _():
        pl.semaphore_signal(barrier, inc=1, device_id={"col": col + CORES})

    @pl.when(has_down)
    def _():
        pl.semaphore_signal(barrier, inc=1, device_id={"col": col - CORES})

    load_a = pltpu.make_async_copy(density, a_full.at[col], load_sem.at[0])
    load_b = pltpu.make_async_copy(response, b_full.at[row], load_sem.at[1])
    load_masks = [
        pltpu.make_async_copy(source, target, load_sem.at[2 + i])
        for i, (source, target) in enumerate((
            (density_mask_in, density_mask), (response_mask_in, response_mask), (filter_mask_in, filter_mask)))
    ]
    load_a.start()
    load_masks[0].start()
    load_masks[1].start()
    load_b.start()
    load_masks[2].start()
    acc[...] = jnp.zeros_like(acc)
    load_a.wait()
    load_masks[0].wait()
    for i in range(rows // blk_r):
        for k in range(kblock // blk_k):
            part = (col, pl.ds(i * blk_r, blk_r), pl.ds(k * blk_k, blk_k))
            factor = jnp.full((blk_r, blk_k), density_mask[k, i].astype(jnp.float32)).astype(jnp.bfloat16)
            a_full[part] = a_full[part] * factor
    load_b.wait()
    load_masks[1].wait()
    load_masks[2].wait()
    for d in range(dirs):
        for i in range(depth // blk_k):
            for k in range(width // blk_k):
                part = (row, d, pl.ds(i * blk_k, blk_k), pl.ds(k * blk_k, blk_k))
                factor = jnp.full((blk_k, blk_k), response_mask[d, k, i].astype(jnp.float32)).astype(jnp.bfloat16)
                b_full[part] = b_full[part] * factor
    pl.semaphore_wait(barrier, 3 + has_up.astype(jnp.int32) + has_down.astype(jnp.int32))

    def a_copy(way, item):
        step, half = item // PIECES, item % PIECES
        sign = 1 - 2 * way
        origin = (chip - sign * step) * CORES + core
        ref = a_full.at[origin, pl.ds(pl.multiple_of(half * piece, piece), piece)]
        return pltpu.make_async_remote_copy(
            ref, ref, a_send.at[way, item], a_recv.at[way, item],
            device_id={"col": col + sign * CORES},
        )

    def a_arrival(way, item):
        step, half = item // PIECES, item % PIECES
        sign = 1 - 2 * way
        origin = (chip - sign * (step + 1)) * CORES + core
        ref = a_full.at[origin, pl.ds(pl.multiple_of(half * piece, piece), piece)]
        return pltpu.make_async_remote_copy(
            ref, ref, a_send.at[way, item], a_recv.at[way, item],
            device_id={"col": col + sign * CORES},
        )

    def d_copy(origin_chip, half, whose):
        ref = a_full.at[origin_chip * CORES + whose, pl.ds(pl.multiple_of(half * piece, piece), piece)]
        return pltpu.make_async_remote_copy(
            ref, ref, d_send.at[origin_chip, half], d_recv.at[origin_chip, half],
            device_id={"col": partner},
        )

    def b_ref(way, item, origin_pos):
        j = item % nb
        d, s = j // (per * SPLIT), j % (per * SPLIT)
        if way == 1:
            d = dirs - 1 - d
        return b_full.at[row_of(origin_pos), d, pl.ds(pl.multiple_of(s * thin, thin), thin)]

    def b_copy(way, item):
        sign = 1 - 2 * way
        ref = b_ref(way, item, pos - sign * (item // nb))
        return pltpu.make_async_remote_copy(
            ref, ref, b_send.at[way, item], b_recv.at[way, item],
            device_id={"row": next_row if way == 0 else prev_row},
        )

    def b_arrival(way, item):
        sign = 1 - 2 * way
        ref = b_ref(way, item, pos - sign * (item // nb + 1))
        return pltpu.make_async_remote_copy(
            ref, ref, b_send.at[way, item], b_recv.at[way, item],
            device_id={"row": next_row if way == 0 else prev_row},
        )

    own_b = min(nb, b_items)
    for item in range(max(own_b, PIECES)):
        if item < PIECES and chips > 1:
            pl.when(has_up)(lambda item=item: a_copy(0, item).start())
            pl.when(has_down)(lambda item=item: a_copy(1, item).start())
        if item < own_b:
            b_copy(0, item).start()
            b_copy(1, item).start()
    for half in range(PIECES):
        d_copy(chip, half, core).start()

    def ready(origin_chip, c, d, source, s):
        late = jnp.where(c == core, 0, 1)
        t_a = PIECES * jnp.abs(origin_chip - chip) + late
        gap = lax.rem(pos - pos_of(source) + ring, ring)
        from_prev = (gap - 1) * nb + (d * per + s + 1) * SPLIT
        from_next = (ring - gap - 1) * nb + ((dirs - 1 - d) * per + s + 1) * SPLIT
        up = jnp.logical_or(gap < far, jnp.logical_and(gap == far, d < dirs // 2))
        t_b = jnp.where(gap == 0, 0, jnp.where(up, from_prev, from_next))
        return jnp.maximum(t_a, t_b)

    def compute(tick):
        def unit(index, carry):
            d, k = index % dirs, index // dirs
            o, c = k // CORES, k % CORES
            source, s = k // per, k % per

            @pl.when(ready(o, c, d, source, s) == tick)
            def _():
                acc[d] += jnp.dot(
                    a_full[k],
                    b_full[source, d, pl.ds(pl.multiple_of(s * kblock, kblock), kblock)],
                    preferred_element_type=jnp.float32,
                )
            return carry

        lax.fori_loop(0, cols * dirs, unit, 0)

    ticks = max(a_items + 1, b_items)

    def arrives(way, item):
        origin = chip - (1 - 2 * way) * (item // PIECES + 1)
        inside = jnp.logical_and(origin >= 0, origin < chips)
        return origin, jnp.logical_and(jnp.logical_and(item >= 0, item < a_items), inside)

    def step(tick, carry):
        item = tick - 1
        for way in range(2):
            origin, here = arrives(way, item)

            @pl.when(here)
            def _():
                a_arrival(way, item).wait_recv()

                @pl.when(has_up if way == 0 else has_down)
                def _():
                    a_copy(way, item + PIECES).start()

                d_copy(origin, item % PIECES, core).start()

        @pl.when(jnp.logical_and(item >= 0, item < b_items))
        def _():
            for way in range(2):
                b_arrival(way, item).wait_recv()

                @pl.when(item + nb < b_items)
                def _():
                    b_copy(way, item + nb).start()

        for way in range(2):
            origin, here = arrives(way, item - 1)

            @pl.when(here)
            def _():
                d_copy(origin, (item - 1) % PIECES, CORES - 1 - core).wait_recv()

        @pl.when(tick == 1)
        def _():
            for part in range(PIECES):
                d_copy(chip, part, CORES - 1 - core).wait_recv()

        compute(tick)
        return carry

    lax.fori_loop(0, ticks + 1, step, 0)

    blk_m, blk_n = rows // filter_mask.shape[1], width // filter_mask.shape[0]
    for d in range(dirs):
        for i in range(rows // blk_m):
            for k in range(width // blk_n):
                part = (d, pl.ds(i * blk_m, blk_m), pl.ds(k * blk_n, blk_n))
                out[part] = (acc[part] * filter_mask[k, i].astype(jnp.float32)).astype(jnp.bfloat16)

    def drain_a(item, carry):
        for way in range(2):
            sign = 1 - 2 * way
            origin = chip - sign * (item // PIECES)
            sent = jnp.logical_and(has_up if way == 0 else has_down, jnp.logical_and(origin >= 0, origin < chips))
            pl.when(sent)(lambda way=way: a_copy(way, item).wait_send())
        return carry

    def drain_b(item, carry):
        for way in range(2):
            b_copy(way, item).wait_send()
        return carry

    def drain_d(index, carry):
        d_copy(index // PIECES, index % PIECES, core).wait_send()
        return carry

    lax.fori_loop(0, a_items, drain_a, 0)
    lax.fori_loop(0, b_items, drain_b, 0)
    lax.fori_loop(0, chips * PIECES, drain_d, 0)


def solution(mesh):
    ring, cols = mesh.shape["row"], mesh.shape["col"]

    def body(density, density_mask, response, response_mask, filter_mask):
        dirs, depth, width = response.shape
        rows, kblock = density.shape
        chips = cols // CORES
        nb = dirs * (depth // kblock) * SPLIT
        a_items = PIECES * (chips - 1)
        b_items = nb * (ring // 2 - 1) + nb // 2
        dma = pltpu.SemaphoreType.DMA
        hbm = pl.BlockSpec(memory_space=pl.ANY)
        masks = (density_mask.T, jnp.swapaxes(response_mask, 1, 2), filter_mask.T)
        return pl.pallas_call(
            functools.partial(kernel, ring, cols),
            out_shape=pltpu.VMEM((dirs, rows, width), jnp.bfloat16),
            in_specs=[hbm] * 5,
            out_specs=pl.BlockSpec(memory_space=pltpu.VMEM),
            scratch_shapes=[
                *(pltpu.SMEM(mask.shape, mask.dtype) for mask in masks),
                pltpu.VMEM((cols, rows, kblock), jnp.bfloat16),
                pltpu.VMEM((ring, dirs, depth, width), jnp.bfloat16),
                pltpu.VMEM((dirs, rows, width), jnp.float32),
                dma((5,)),
                dma((2, a_items)),
                dma((2, a_items)),
                dma((2, b_items)),
                dma((2, b_items)),
                dma((chips, PIECES)),
                dma((chips, PIECES)),
            ],
            compiler_params=pltpu.CompilerParams(collective_id=0, has_side_effects=True),
        )(density, masks[0], response, masks[1], masks[2])

    return jax.shard_map(
        body,
        mesh=mesh,
        in_specs=(P("row", "col"), P("row", "col"), P(None, "row", "col"), P(None, "row", "col"), P("row", "col")),
        out_specs=P(None, "row", "col"),
        check_vma=False,
    )
```

time: 26.9 us -> 26.7 us (level); the launches traced: 26.7 us -> 26.2 us
  Pallas kernels: 25.9 us -> 25.4 us
    pallas_call x1, Pallas kernels: 25.9 us -> 25.4 us  [body(): pl.pallas_call(functools.partial(kernel, ring, cols), out_shape=pltpu.VME...]
where the time goes in v3:
time: 26.7 us; the launch traced here: 26.2 us
  Pallas kernels  25.4 us (95%)
  local copies, waits for them, and re-layouts  0.8 us (3%)
    pallas_call x1, Pallas kernels, body(): pl.pallas_call(functools.partial(kernel, ring, cols), out_shape=pltpu.VME...  25.4 us
    unnamed x1, local copies, waits for them, and re-layouts  0.8 us

profile of v3, /device:TPU:1, one launch (start us, length us, event | category | flops | bytes accessed | tf_op | source)
XLA Modules:
  0.0 26.2 jit_solution(5652013958544678946)
XLA Ops:
  0.0 25.4 %shard_map.55 = bf16[2,512,256]{2,1,0:T(8,128)(2,1)S(1)} custom-call(bf16[512,256]{1,0:T(8,128)(2,1)} %density.1, s32[2,4]{1,0:T(2,128)} %bitcast.4, bf16[2,512,256]{2,1,0:T(8,128)(2,1)} %response.1, s32[2,2,4]{2,1,0:T(2,128)} %bitcast.3, s32[2,4]{1,0:T(2,128)} %bitcast.5), custom_call_target="tpu_custom_call" | custom-call | tf_op jit(solution)/shard_map/pallas_call | solution.py:271
  25.4 0.8 %copy.7 = bf16[2,512,256]{2,1,0:T(8,128)(2,1)} copy(bf16[2,512,256]{2,1,0:T(8,128)(2,1)S(1)} %shard_map.55) | data formatting | bytes 1048576

commit v4 on v3

--- a/solution.py
+++ b/solution.py
@@ -8,8 +8,9 @@
 from jax.sharding import PartitionSpec as P
 
 CORES = 2
-PIECES = 4
+PIECES = 2
 SPLIT = 2
+RATIO = PIECES // SPLIT
 
 
 def kernel(
@@ -22,8 +23,8 @@
     rows, kblock = density.shape
     piece = rows // PIECES
     per = depth // kblock
-    thin = kblock // SPLIT
-    nb = dirs * per * SPLIT
+    thin = depth // SPLIT
+    nb = dirs * SPLIT
     far = ring // 2
     a_items = PIECES * (chips - 1)
     b_items = nb * (far - 1) + nb // 2
@@ -119,7 +120,7 @@
 
     def b_ref(way, item, origin_pos):
         j = item % nb
-        d, s = j // (per * SPLIT), j % (per * SPLIT)
+        d, s = j // SPLIT, j % SPLIT
         if way == 1:
             d = dirs - 1 - d
         return b_full.at[row_of(origin_pos), d, pl.ds(pl.multiple_of(s * thin, thin), thin)]
@@ -155,30 +156,29 @@
         late = jnp.where(c == core, 0, 1)
         t_a = PIECES * jnp.abs(origin_chip - chip) + late
         gap = lax.rem(pos - pos_of(source) + ring, ring)
-        from_prev = (gap - 1) * nb + (d * per + s + 1) * SPLIT
-        from_next = (ring - gap - 1) * nb + ((dirs - 1 - d) * per + s + 1) * SPLIT
-        up = jnp.logical_or(gap < far, jnp.logical_and(gap == far, d < dirs // 2))
-        t_b = jnp.where(gap == 0, 0, jnp.where(up, from_prev, from_next))
+        last = ((s + 1) * kblock - 1) // thin + 1
+        from_prev = (gap - 1) * nb + d * SPLIT + last
+        from_next = (ring - gap - 1) * nb + (dirs - 1 - d) * SPLIT + last
+        up = gap <= far if d < dirs // 2 else gap < far
+        t_b = RATIO * jnp.where(gap == 0, 0, jnp.where(up, from_prev, from_next))
         return jnp.maximum(t_a, t_b)
 
+    units = []
+    for k in range(cols):
+        for d in range(dirs):
+            source, s = k // per, k % per
+            units.append((k, d, source, s, ready(k // CORES, k % CORES, d, source, s)))
+
     def compute(tick):
-        def unit(index, carry):
-            d, k = index % dirs, index // dirs
-            o, c = k // CORES, k % CORES
-            source, s = k // per, k % per
-
-            @pl.when(ready(o, c, d, source, s) == tick)
+        for k, d, source, s, due in units:
+
+            @pl.when(due == tick)
             def _():
                 acc[d] += jnp.dot(
-                    a_full[k],
-                    b_full[source, d, pl.ds(pl.multiple_of(s * kblock, kblock), kblock)],
-                    preferred_element_type=jnp.float32,
+                    a_full[k], b_full[source, d, pl.ds(s * kblock, kblock)], preferred_element_type=jnp.float32
                 )
-            return carry
-
-        lax.fori_loop(0, cols * dirs, unit, 0)
-
-    ticks = max(a_items + 1, b_items)
+
+    ticks = max(a_items + 1, RATIO * b_items)
 
     def arrives(way, item):
         origin = chip - (1 - 2 * way) * (item // PIECES + 1)
@@ -200,14 +200,16 @@
 
                 d_copy(origin, item % PIECES, core).start()
 
-        @pl.when(jnp.logical_and(item >= 0, item < b_items))
+        b_item = tick // RATIO - 1
+
+        @pl.when(jnp.logical_and(tick % RATIO == 0, jnp.logical_and(b_item >= 0, b_item < b_items)))
         def _():
             for way in range(2):
-                b_arrival(way, item).wait_recv()
-
-                @pl.when(item + nb < b_items)
+                b_arrival(way, b_item).wait_recv()
+
+                @pl.when(b_item + nb < b_items)
                 def _():
-                    b_copy(way, item + nb).start()
+                    b_copy(way, b_item + nb).start()
 
         for way in range(2):
             origin, here = arrives(way, item - 1)
@@ -262,7 +264,7 @@
         dirs, depth, width = response.shape
         rows, kblock = density.shape
         chips = cols // CORES
-        nb = dirs * (depth // kblock) * SPLIT
+        nb = dirs * SPLIT
         a_items = PIECES * (chips - 1)
         b_items = nb * (ring // 2 - 1) + nb // 2
         dma = pltpu.SemaphoreType.DMA

time: 26.7 us -> 25.1 us (0.940); the launches traced: 26.2 us -> 25 us
  Pallas kernels: 25.4 us -> 24.2 us
    pallas_call x1, Pallas kernels: 25.4 us -> 24.2 us  [body(): pl.pallas_call(functools.partial(kernel, ring, cols), out_shape=pltpu.VME...]
where the time goes in v4:
time: 25.1 us; the launch traced here: 25 us
  Pallas kernels  24.2 us (96%)
  local copies, waits for them, and re-layouts  0.8 us (3%)
    pallas_call x1, Pallas kernels, body(): pl.pallas_call(functools.partial(kernel, ring, cols), out_shape=pltpu.VME...  24.2 us
    unnamed x1, local copies, waits for them, and re-layouts  0.8 us

profile of v4, /device:TPU:1, one launch (start us, length us, event | category | flops | bytes accessed | tf_op | source)
XLA Modules:
  0.0 25.0 jit_solution(5422968534301898306)
XLA Ops:
  0.0 24.2 %shard_map.55 = bf16[2,512,256]{2,1,0:T(8,128)(2,1)S(1)} custom-call(bf16[512,256]{1,0:T(8,128)(2,1)} %density.1, s32[2,4]{1,0:T(2,128)} %bitcast.4, bf16[2,512,256]{2,1,0:T(8,128)(2,1)} %response.1, s32[2,2,4]{2,1,0:T(2,128)} %bitcast.3, s32[2,4]{1,0:T(2,128)} %bitcast.5), custom_call_target="tpu_custom_call" | custom-call | tf_op jit(solution)/shard_map/pallas_call | solution.py:273
  24.2 0.8 %copy.7 = bf16[2,512,256]{2,1,0:T(8,128)(2,1)} copy(bf16[2,512,256]{2,1,0:T(8,128)(2,1)S(1)} %shard_map.55) | data formatting | bytes 1048576
